TPU v7x, 256 devices: a 8x8x2 block of a 8x8x16 slice. The times are simulated.
256 devices in a mesh: grp: 2 (over z), kvp: 16 (over x, core), tp: 8 (over y).
Axes of the slice: x: 8, y: 8, z: 2, core: 2. Of those that a mesh axis runs over, the one named last changes fastest.
The devices are a block of a 8x8x16 slice.
Arguments:
- hidden_in: bfloat16 [16, 7168], P('grp'), parts along dimension 0, may hold values from -3 to 3
- queries_nope: bfloat16 [16, 128, 128], P('grp', ('kvp', 'tp')), parts along dimension 0, may hold values from -6 to 6
- queries_rope: bfloat16 [16, 128, 64], P('grp', ('kvp', 'tp')), parts along dimension 0, may hold values from -26 to 26
- cache: bfloat16 [16, 6144, 576], P('grp', 'kvp'), parts along dimension 0, may hold values from -20 to 20
- lengths: int32 [16], P('grp'), parts along dimension 0, may hold values from 128 to 6144, as said below
- w_uk: bfloat16 [128, 128, 512], P(('kvp', 'tp')), may hold values from -0.5 to 0.5
- w_uv: bfloat16 [128, 512, 128], P(('kvp', 'tp')), may hold values from -0.25 to 0.25
- w_out: bfloat16 [16384, 7168], P(('kvp', 'tp')), may hold values from -0.1875 to 0.1875
- norm_gain: float32 [7168], replicated, may hold values from 0.25 to 1.75
- w_gate: bfloat16 [7168, 18432], P(None, ('kvp', 'tp')), may hold values from -0.0625 to 0.0625
- w_up: bfloat16 [7168, 18432], P(None, ('kvp', 'tp')), may hold values from -0.0625 to 0.0625
- w_down: bfloat16 [18432, 7168], P(('kvp', 'tp')), may hold values from -0.15625 to 0.15625
Outputs:
- layer_out: bfloat16 [16, 7168], P('grp', ('kvp', 'tp')), parts along dimension 0
There are 2 independent parts, one for each index of `grp`. A program takes and returns all parts, laid end to end along the dimension named above; an argument that names none is the same for every part. Nothing has to cross between parts.
Inputs may be any that keep to these rules, and one draw needn't show every extreme that they name: `lengths`: every length is a multiple of 128; in every draw some request has the full 6144.
All inputs are finite; a program needn't handle non-finite values.
Results may differ from a plain program's by a relative error of at most 0.04.
Values may be sent and summed in bfloat16 or wider, within the bound.
A program may use at most 64 MiB of HBM per device.

v0:
```python
import jax
import jax.numpy as jnp
from jax import lax
from jax.sharding import Mesh
from jax.sharding import PartitionSpec as P

KVP = ("kvp_0", "kvp_1")
KVP_TP = ("kvp_0", "kvp_1", "tp")


def in_one_piece(arrays, axis, dim, along):
    both = jnp.concatenate(arrays, axis=along)
    whole, at, gathered = (lax.all_gather(both, axis, axis=dim, tiled=True), 0, [])
    for a in arrays:
        gathered.append(lax.slice_in_dim(whole, at, at + a.shape[along], axis=along))
        at += a.shape[along]
    return tuple(gathered)


def sum_in_order(blocks, axes, sequence):
    inside = blocks.shape[1:]
    blocks = blocks.reshape(*(lax.axis_size(a) for a in axes), *inside)
    blocks = jnp.moveaxis(blocks, sequence, range(len(axes))).reshape(-1, *inside)
    for k in sequence:
        blocks = lax.psum_scatter(blocks, axes[k], scatter_dimension=0, tiled=True)
    return blocks[0]


def in_blocks(value, dim, size):
    dims = value.shape
    blocks = value.reshape(*dims[:dim], size, dims[dim] // size, *dims[dim + 1 :])
    return jnp.moveaxis(blocks, dim, 0)


def sum_by_axis(value, axes, sequence, dim):
    size = lax.axis_size(axes)
    return sum_in_order(in_blocks(value, dim, size), axes, sequence)


def project(o_lat, w_uv, w_out):
    head_out = jnp.einsum("bhl,hle->bhe", o_lat, w_uv, preferred_element_type=jnp.float32).astype(
        jnp.bfloat16
    )
    return jnp.dot(
        head_out.reshape(head_out.shape[0], -1), w_out, preferred_element_type=jnp.float32
    )


def per_device(
    hidden_in,
    queries_nope,
    queries_rope,
    cache,
    lengths,
    w_uk,
    w_uv,
    w_out,
    norm_gain,
    w_gate,
    w_up,
    w_down,
):
    batch, heads_dev, head_dim = queries_nope.shape
    latent = w_uk.shape[2]
    ctx_dev = cache.shape[1]
    groups = lax.axis_size(KVP)
    score_scale = float(head_dim + queries_rope.shape[2]) ** (-0.5)
    q_lat = jnp.einsum(
        "bhd,hdl->bhl", queries_nope, w_uk, preferred_element_type=jnp.float32
    ).astype(jnp.bfloat16)
    q_lat_all, rope_all = in_one_piece((q_lat, queries_rope), KVP, 1, 2)
    q_full = jnp.concatenate([q_lat_all, rope_all], axis=2)
    scores = (
        jnp.einsum("bhc,btc->bht", q_full, cache, preferred_element_type=jnp.float32) * score_scale
    )
    offset = lax.axis_index(KVP) * ctx_dev
    visible = ((offset + jnp.arange(ctx_dev, dtype=jnp.int32))[None, :] < lengths[:, None])[
        :, None, :
    ]
    masked = jnp.where(visible, scores, jnp.float32(-1e30))
    block_max = jnp.max(masked, axis=2)
    exponent = jnp.where(visible, jnp.exp(masked - block_max[..., None]), jnp.float32(0.0))
    guarded = jnp.maximum(jnp.sum(exponent, axis=2), 1.0)
    log_total = block_max + jnp.log(guarded)
    weights = (exponent / guarded[..., None]).astype(jnp.bfloat16)
    partial_value = jnp.einsum("bht,btc->bhc", weights, cache, preferred_element_type=jnp.float32)[
        ..., :latent
    ]
    blocks = partial_value.reshape(batch, groups, heads_dev, latent)
    block_logs = log_total.reshape(batch, groups, heads_dev)
    part_blocks = lax.all_to_all(
        blocks.astype(jnp.bfloat16), KVP, split_axis=1, concat_axis=1, tiled=True
    ).astype(blocks.dtype)
    part_logs = lax.all_to_all(
        block_logs.astype(jnp.bfloat16), KVP, split_axis=1, concat_axis=1, tiled=True
    ).astype(block_logs.dtype)
    highest = jnp.max(part_logs, axis=1)
    overall = highest + jnp.log(jnp.sum(jnp.exp(part_logs - highest[:, None, :]), axis=1))
    scaled = jnp.exp(part_logs - overall[:, None, :])[..., None] * part_blocks
    o_lat = jnp.sum(scaled, axis=1).astype(jnp.bfloat16)
    attention = project(o_lat, w_uv, w_out)
    model_width = norm_gain.shape[0]
    share_width = model_width // lax.axis_size(KVP_TP)
    share_start = lax.axis_index(KVP_TP) * share_width
    attn_whole = lax.psum(attention, KVP_TP)
    residual = hidden_in.astype(jnp.float32) + attn_whole
    mean_square = jnp.mean(residual * residual, axis=1)
    normed = (residual * lax.rsqrt(mean_square + 1e-06)[:, None] * norm_gain[None, :]).astype(
        jnp.bfloat16
    )
    residual_share = lax.dynamic_slice_in_dim(residual, share_start, share_width, 1)
    gate_proj = jnp.dot(normed, w_gate, preferred_element_type=jnp.float32)
    up_proj = jnp.dot(normed, w_up, preferred_element_type=jnp.float32)
    act = (jax.nn.silu(gate_proj) * up_proj).astype(jnp.bfloat16)
    ffn_terms = jnp.dot(act, w_down, preferred_element_type=jnp.float32)
    ffn_share = sum_by_axis(ffn_terms, KVP_TP, (1, 0, 2), 1)
    return (residual_share + ffn_share).astype(jnp.bfloat16)


def solution(mesh):
    torus = Mesh(
        mesh.devices.reshape(mesh.shape["grp"], 8, 2, mesh.shape["tp"]),
        ("grp", "kvp_0", "kvp_1", "tp"),
    )
    return jax.shard_map(
        per_device,
        mesh=torus,
        in_specs=(
            P("grp", None),
            P("grp", KVP_TP, None),
            P("grp", KVP_TP, None),
            P("grp", KVP, None),
            P("grp"),
            P(KVP_TP, None, None),
            P(KVP_TP, None, None),
            P(KVP_TP, None),
            P(),
            P(None, KVP_TP),
            P(None, KVP_TP),
            P(KVP_TP, None),
        ),
        out_specs=P("grp", KVP_TP),
        check_vma=False,
    )
```

profile of v0, /device:TPU:514, one launch (start us, length us, event | category | flops | bytes accessed | tf_op | source)
XLA Modules:
  0.0 365.7 jit_solution(1368219524394948218)
XLA Ops:
  6.6 1.2 fusion.1
  7.7 0.7 pad_maximum_fusion
  8.4 34.0 %all_gather.3 = bf16[8,16,576]{2,0,1:T(8,128)(2,1)S(1)} all-gather(bf16[8,1,576]{2,0,1:T(8,128)(2,1)S(1)} %pad_maximum_fusion), channel_id=1, replica_groups=mesh['grp'=2,'kvp_0'=8,'kvp_1'=2,'tp'=8] {'kvp_0','kvp_1'}, dimensions={1}, use_global_device_ids=true | all-gather | bytes 156672 | tf_op jit(solution)/shard_map/all_gather | solution.py:13
  42.4 0.7 broadcast_compare_fusion
  43.1 0.7 fusion.35
  43.8 0.7 copy-done.2
  44.5 0.2 fusion.6
  44.7 0.6 fusion.30
  45.3 0.7 copy.24
  45.9 3.6 all-to-all-start
  49.5 2.0 fusion.11
  51.6 0.7 copy.27
  52.3 3.4 all-to-all-done
  55.7 5.4 %all-to-all-start.1 = ((bf16[8,16,1,512]{3,0,2,1:T(8,128)(2,1)}), bf16[8,16,1,512]{3,0,2,1:T(8,128)(2,1)}, u32[]{:S(2)}, u32[]{:S(2)}) async-start(bf16[8,16,1,512]{3,0,2,1:T(8,128)(2,1)} %copy.27), calls=%async_computation.1 | async-start | bytes 262144 | tf_op jit(solution)/shard_map/all_to_all | solution.py:91
  61.2 0.5 reduce_max.25
  61.7 0.1 copy.25
  61.8 0.8 fusion.24
  62.8 5.9 %all-to-all-done.1 = bf16[8,16,1,512]{3,0,2,1:T(8,128)(2,1)} async-done(((bf16[8,16,1,512]{3,0,2,1:T(8,128)(2,1)}), bf16[8,16,1,512]{3,0,2,1:T(8,128)(2,1)}, u32[]{:S(2)}, u32[]{:S(2)}) %all-to-all-start.1) | async-done | bytes 131104 | tf_op jit(solution)/shard_map/all_to_all | solution.py:91
  68.7 1.0 multiply_reduce_fusion
  69.7 2.7 fusion.4
  72.5 185.7 %all-reduce.3.cloned.1.call-done = f32[8,7168]{1,0:T(8,128)} async-done(((f32[8,7168]{1,0:T(8,128)}), f32[8,7168]{1,0:T(8,128)}) %all-reduce.3.cloned.1.call-update) | async-done | bytes 229392 | tf_op jit(solution)/shard_map/psum | solution.py:105
  258.3 1.2 multiply_reduce_fusion.1
  259.5 0.7 copy-done.1
  260.2 2.3 fusion.34
  262.4 4.6 %fusion.3 = f32[8,7168]{1,0:T(8,128)} fusion(bf16[144,7168]{1,0:T(8,128)(2,1)} %param.23, bf16[7168,144]{0,1:T(8,128)(2,1)} %param.22, f32[8,144]{1,0:T(8,128)S(1)} %fusion.34, f32[8,7168]{1,0:T(8,128)} %copy-done.1, f32[7168]{0:T(1024)} %param.20, f32[8]{0:T(128)S(1)} %add_rsqrt_fusion), kind=kOutput, calls=%fused_computation.6 | convolution fusion | flops 33209088 | bytes 4620832 | tf_op jit(solution)/shard_map/dot_general | solution.py:115
  267.1 2.2 reshape.125
  269.3 2.2 copy.29
  271.5 12.6 %reduce-scatter.3.cloned.1.call-done = f32[64,8,56]{2,1,0:T(8,128)} async-done(((f32[128,8,56]{2,1,0:T(8,128)}), f32[64,8,56]{2,1,0:T(8,128)}) %reduce-scatter.3.cloned.1.call-update) | async-done | bytes 114704 | tf_op jit(solution)/shard_map/reduce_scatter | solution.py:25
  284.3 0.6 dynamic-slice
  284.8 41.0 %reduce-scatter.5.cloned.1.call-done = f32[8,8,56]{2,1,0:T(8,128)} async-done(((f32[64,8,56]{2,1,0:T(8,128)}), f32[8,8,56]{2,1,0:T(8,128)}) %reduce-scatter.5.cloned.1.call-update) | async-done | bytes 14352 | tf_op jit(solution)/shard_map/reduce_scatter | solution.py:25
  325.8 31.4 %all-reduce = f32[8,8,56]{2,1,0:T(8,128)} all-reduce(f32[8,8,56]{2,1,0:T(8,128)} %reduce-scatter.5.cloned.1.call-done), channel_id=4, replica_groups=mesh['grp'=2,'kvp_0'=8,'kvp_1'=2,'tp'=8] {'tp'}, use_global_device_ids=true, to_apply=%region_9.10.clone | all-reduce | flops 3584 | bytes 28672
  357.3 1.9 fusion.28
  (19 shorter events, 0.6 us)
Async XLA Ops:
  6.5 36.6 %copy-start = (bf16[8,384,576]{1,2,0:T(8,128)(2,1)S(1)}, bf16[8,384,576]{1,2,0:T(8,128)(2,1)}, u32[]{:S(2)}) copy-start(bf16[8,384,576]{1,2,0:T(8,128)(2,1)} %param.15) | copy-start | bytes 10616836
  43.8 0.7 copy-start.2
  45.9 9.8 %all-to-all-start = ((bf16[8,16,1]{0,2,1:T(2,128)(2,1)}), bf16[8,16,1]{0,2,1:T(2,128)(2,1)S(1)}, u32[]{:S(2)}, u32[]{:S(2)}) async-start(bf16[8,16,1]{0,2,1:T(2,128)(2,1)} %copy.24), calls=%async_computation | async-start | bytes 16384 | tf_op jit(solution)/shard_map/all_to_all | solution.py:94
  55.7 12.9 %all-to-all-start.1 = ((bf16[8,16,1,512]{3,0,2,1:T(8,128)(2,1)}), bf16[8,16,1,512]{3,0,2,1:T(8,128)(2,1)}, u32[]{:S(2)}, u32[]{:S(2)}) async-start(bf16[8,16,1,512]{3,0,2,1:T(8,128)(2,1)} %copy.27), calls=%async_computation.1 | async-start | bytes 262144 | tf_op jit(solution)/shard_map/all_to_all | solution.py:91
  61.1 197.2 %all-reduce.3.cloned.1.call-start = ((), (), s32[]{:S(2)}) async-start(), calls=%async_computation.4 | async-start | bytes 458752 | tf_op jit(solution)/shard_map/psum | solution.py:105
  72.5 211.7 %reduce-scatter.3.cloned.1.call-start = ((), (), s32[]{:S(2)}) async-start(), calls=%async_computation.5 | async-start | bytes 786432 | tf_op jit(solution)/shard_map/reduce_scatter | solution.py:25
  259.5 0.7 copy-start.1
  267.1 17.2 %copy-start.3 = (u32[256]{0:T(256)S(1)}, u32[256]{0:T(256)}, u32[]{:S(2)}) copy-start(u32[256]{0:T(256)} %constant.55) | copy-start | bytes 3076
  271.5 54.4 %reduce-scatter.5.cloned.1.call-start = ((), (), s32[]{:S(2)}) async-start(), calls=%async_computation.6 | async-start | bytes 294912 | tf_op jit(solution)/shard_map/reduce_scatter | solution.py:25
Sparse Core Ops, SparseCore 0:
  72.6 185.6 all-reduce.2
  271.6 12.5 reduce-scatter.2
  286.7 39.0 reduce-scatter.4
where the time goes:
time: 366 us
  waiting for transfers between devices  249 us (68%)
  blocking collectives  65.4 us (18%)
  matrix products  13.5 us (4%)
  between operations  13.2 us (4%)
  starting transfers between devices  9.14 us (2%)
  local copies, waits for them, and re-layouts  7.86 us (2%)
  other arithmetic  7.76 us (2%)
    psum x1, waiting for transfers between devices, per_device(): attn_whole = lax.psum(attention, KVP_TP)  186 us
    reduce_scatter x2, waiting for transfers between devices, sum_in_order(): blocks = lax.psum_scatter(blocks, axes[k], scatter_dimension=0, tiled=True)  53.6 us
    all_gather x1, blocking collectives, in_one_piece(): lax.all_gather(both, axis, axis=dim, tiled=True)  34 us
    unnamed x1, blocking collectives  31.4 us
  transfers between devices with their start and end apart: 5, of which 5 were waited for; matrix products, arithmetic and copies ran while one was open for 1% of the time, Pallas kernels for 0%

commit v1 on v0

--- a/solution.py
+++ b/solution.py
@@ -6,6 +6,12 @@
 
 KVP = ("kvp_0", "kvp_1")
 KVP_TP = ("kvp_0", "kvp_1", "tp")
+
+
+def gather_and_add(value, mesh_axis):
+    shards = lax.all_gather(value, mesh_axis, axis=0, tiled=False)
+    total = shards.sum(axis=0)
+    return total
 
 
 def in_one_piece(arrays, axis, dim, along):
@@ -102,7 +108,7 @@
     model_width = norm_gain.shape[0]
     share_width = model_width // lax.axis_size(KVP_TP)
     share_start = lax.axis_index(KVP_TP) * share_width
-    attn_whole = lax.psum(attention, KVP_TP)
+    attn_whole = gather_and_add(attention, KVP_TP)
     residual = hidden_in.astype(jnp.float32) + attn_whole
     mean_square = jnp.mean(residual * residual, axis=1)
     normed = (residual * lax.rsqrt(mean_square + 1e-06)[:, None] * norm_gain[None, :]).astype(

time: 366 us -> 317 us (0.87)
  waiting for transfers between devices: 249 us -> 192 us
  other arithmetic: 7.76 us -> 18 us
    psum x1 -> x0, waiting for transfers between devices: 186 us -> none  [per_device(): attn_whole = lax.psum(attention, KVP_TP)]
    all_gather x0 -> x1, waiting for transfers between devices: none -> 128 us  [gather_and_add(): shards = lax.all_gather(value, mesh_axis, axis=0, tiled=False)]
    reduce_sum x0 -> x1, other arithmetic: none -> 11.2 us  [gather_and_add(): total = shards.sum(axis=0)]
  transfers between devices with their start and end apart: 5 -> 5, of which waited for: 5 -> 5; matrix products, arithmetic and copies ran while one was open for 1% -> 2% of each run, Pallas kernels for 0% -> 0%
where the time goes in v1:
time: 317 us
  waiting for transfers between devices  192 us (61%)
  blocking collectives  65.4 us (21%)
  other arithmetic  18 us (6%)
  between operations  13.2 us (4%)
  matrix products  11.9 us (4%)
  starting transfers between devices  9.14 us (3%)
  local copies, waits for them, and re-layouts  7.87 us (2%)
    all_gather x1, waiting for transfers between devices, gather_and_add(): shards = lax.all_gather(value, mesh_axis, axis=0, tiled=False)  128 us
    reduce_scatter x2, waiting for transfers between devices, sum_in_order(): blocks = lax.psum_scatter(blocks, axes[k], scatter_dimension=0, tiled=True)  54.4 us
    all_gather x1, blocking collectives, in_one_piece(): lax.all_gather(both, axis, axis=dim, tiled=True)  34 us
    unnamed x1, blocking collectives  31.4 us
    reduce_sum x1, other arithmetic, gather_and_add(): total = shards.sum(axis=0)  11.2 us
  transfers between devices with their start and end apart: 5, of which 5 were waited for; matrix products, arithmetic and copies ran while one was open for 2% of the time, Pallas kernels for 0%

profile of v1, /device:TPU:514, one launch (start us, length us, event | category | flops | bytes accessed | tf_op | source)
XLA Modules:
  0.0 317.0 jit_solution(5335259182363710490)
XLA Ops:
  6.6 1.2 fusion.1
  7.7 0.7 pad_maximum_fusion
  8.4 34.0 %all_gather.9 = bf16[8,16,576]{2,0,1:T(8,128)(2,1)S(1)} all-gather(bf16[8,1,576]{2,0,1:T(8,128)(2,1)S(1)} %pad_maximum_fusion), channel_id=1, replica_groups=mesh['grp'=2,'kvp_0'=8,'kvp_1'=2,'tp'=8] {'kvp_0','kvp_1'}, dimensions={1}, use_global_device_ids=true | all-gather | bytes 156672 | tf_op jit(solution)/shard_map/all_gather | solution.py:19
  42.4 0.7 broadcast_compare_fusion
  43.1 0.7 fusion.35
  43.8 0.7 copy-done.3
  44.5 0.2 fusion.6
  44.7 0.6 fusion.30
  45.3 0.7 copy.18
  45.9 3.6 %all-to-all-start = ((bf16[8,16,1]{0,2,1:T(2,128)(2,1)}), bf16[8,16,1]{0,2,1:T(2,128)(2,1)S(1)}, u32[]{:S(2)}, u32[]{:S(2)}) async-start(bf16[8,16,1]{0,2,1:T(2,128)(2,1)} %copy.18), calls=%async_computation | async-start | bytes 16384 | tf_op jit(solution)/shard_map/all_to_all | solution.py:100
  49.5 2.0 fusion.11
  51.6 0.7 copy.21
  52.3 3.4 %all-to-all-done = bf16[8,16,1]{0,2,1:T(2,128)(2,1)S(1)} async-done(((bf16[8,16,1]{0,2,1:T(2,128)(2,1)}), bf16[8,16,1]{0,2,1:T(2,128)(2,1)S(1)}, u32[]{:S(2)}, u32[]{:S(2)}) %all-to-all-start) | async-done | bytes 288 | tf_op jit(solution)/shard_map/all_to_all | solution.py:100
  55.7 5.4 %all-to-all-start.1 = ((bf16[8,16,1,512]{3,0,2,1:T(8,128)(2,1)}), bf16[8,16,1,512]{3,0,2,1:T(8,128)(2,1)}, u32[]{:S(2)}, u32[]{:S(2)}) async-start(bf16[8,16,1,512]{3,0,2,1:T(8,128)(2,1)} %copy.21), calls=%async_computation.1 | async-start | bytes 262144 | tf_op jit(solution)/shard_map/all_to_all | solution.py:97
  61.2 0.5 reduce_max.25
  61.8 0.8 fusion.24
  62.8 5.9 %all-to-all-done.1 = bf16[8,16,1,512]{3,0,2,1:T(8,128)(2,1)} async-done(((bf16[8,16,1,512]{3,0,2,1:T(8,128)(2,1)}), bf16[8,16,1,512]{3,0,2,1:T(8,128)(2,1)}, u32[]{:S(2)}, u32[]{:S(2)}) %all-to-all-start.1) | async-done | bytes 131104 | tf_op jit(solution)/shard_map/all_to_all | solution.py:97
  68.7 1.0 multiply_reduce_fusion
  69.7 2.7 fusion.4
  72.5 127.6 %all-gather.3.cloned.1.call-done = f32[1024,7168]{1,0:T(8,128)} async-done(((f32[8,7168]{1,0:T(8,128)}), f32[1024,7168]{1,0:T(8,128)}) %all-gather.3.cloned.1.call-update) | async-done | bytes 29360144 | tf_op jit(solution)/shard_map/all_gather | solution.py:12
  200.2 11.2 %bitcast_reduce_fusion = f32[8,7168]{1,0:T(8,128)S(1)} fusion(f32[1024,7168]{1,0:T(8,128)} %all-gather.3.cloned.1.call-done), kind=kLoop, calls=%fused_computation | loop fusion | flops 7282688 | bytes 29589504 | tf_op jit(solution)/shard_map/reduce_sum | solution.py:13
  211.4 0.2 multiply_reduce_fusion.1
  211.6 0.7 copy-done.1
  212.3 0.7 fusion.34
  212.9 4.6 %fusion.3 = f32[8,7168]{1,0:T(8,128)} fusion(bf16[144,7168]{1,0:T(8,128)(2,1)} %param.23, bf16[7168,144]{0,1:T(8,128)(2,1)} %param.22, f32[8,144]{1,0:T(8,128)S(1)} %fusion.34, f32[8,7168]{1,0:T(8,128)} %copy-done.1, f32[7168]{0:T(1024)} %param.20, f32[8]{0:T(128)S(1)} %add_rsqrt_fusion), kind=kOutput, calls=%fused_computation.7 | convolution fusion | flops 33209088 | bytes 4620832 | tf_op jit(solution)/shard_map/dot_general | solution.py:121
  217.6 2.2 reshape.125
  219.8 2.2 copy.22
  222.1 13.4 %reduce-scatter.3.cloned.1.call-done = f32[64,8,56]{2,1,0:T(8,128)} async-done(((f32[128,8,56]{2,1,0:T(8,128)}), f32[64,8,56]{2,1,0:T(8,128)}) %reduce-scatter.3.cloned.1.call-update) | async-done | bytes 114704 | tf_op jit(solution)/shard_map/reduce_scatter | solution.py:31
  235.6 0.6 dynamic-slice
  236.1 41.0 %reduce-scatter.5.cloned.1.call-done = f32[8,8,56]{2,1,0:T(8,128)} async-done(((f32[64,8,56]{2,1,0:T(8,128)}), f32[8,8,56]{2,1,0:T(8,128)}) %reduce-scatter.5.cloned.1.call-update) | async-done | bytes 14352 | tf_op jit(solution)/shard_map/reduce_scatter | solution.py:31
  277.1 31.4 %all-reduce = f32[8,8,56]{2,1,0:T(8,128)} all-reduce(f32[8,8,56]{2,1,0:T(8,128)} %reduce-scatter.5.cloned.1.call-done), channel_id=5, replica_groups=mesh['grp'=2,'kvp_0'=8,'kvp_1'=2,'tp'=8] {'tp'}, use_global_device_ids=true, to_apply=%region_9.10.clone | all-reduce | flops 3584 | bytes 28672
  308.5 1.9 fusion.28
  (26 shorter events, 0.7 us)
Async XLA Ops:
  6.5 36.6 %copy-start = (bf16[8,384,576]{1,2,0:T(8,128)(2,1)S(1)}, bf16[8,384,576]{1,2,0:T(8,128)(2,1)}, u32[]{:S(2)}) copy-start(bf16[8,384,576]{1,2,0:T(8,128)(2,1)} %param.15) | copy-start | bytes 10616836
  43.8 0.7 copy-start.3
  45.9 9.8 %all-to-all-start = ((bf16[8,16,1]{0,2,1:T(2,128)(2,1)}), bf16[8,16,1]{0,2,1:T(2,128)(2,1)S(1)}, u32[]{:S(2)}, u32[]{:S(2)}) async-start(bf16[8,16,1]{0,2,1:T(2,128)(2,1)} %copy.18), calls=%async_computation | async-start | bytes 16384 | tf_op jit(solution)/shard_map/all_to_all | solution.py:100
  55.7 12.9 %all-to-all-start.1 = ((bf16[8,16,1,512]{3,0,2,1:T(8,128)(2,1)}), bf16[8,16,1,512]{3,0,2,1:T(8,128)(2,1)}, u32[]{:S(2)}, u32[]{:S(2)}) async-start(bf16[8,16,1,512]{3,0,2,1:T(8,128)(2,1)} %copy.21), calls=%async_computation.1 | async-start | bytes 262144 | tf_op jit(solution)/shard_map/all_to_all | solution.py:97
  61.1 139.1 %all-gather.3.cloned.1.call-start = ((), (), s32[]{:S(2)}) async-start(), calls=%async_computation.6 | async-start | bytes 29589504 | tf_op jit(solution)/shard_map/all_gather | solution.py:12
  72.5 163.0 %reduce-scatter.3.cloned.1.call-start = ((), (), s32[]{:S(2)}) async-start(), calls=%async_computation.4 | async-start | bytes 786432 | tf_op jit(solution)/shard_map/reduce_scatter | solution.py:31
  200.2 11.2 %copy-start.4 = (bf16[8,7168]{1,0:T(8,128)(2,1)S(1)}, bf16[8,7168]{1,0:T(8,128)(2,1)}, u32[]{:S(2)}) copy-start(bf16[8,7168]{1,0:T(8,128)(2,1)} %param.12) | copy-start | bytes 344068
  200.2 12.1 %copy-start.2 = (bf16[7168,144]{0,1:T(8,128)(2,1)S(1)}, bf16[7168,144]{0,1:T(8,128)(2,1)}, u32[]{:S(2)}) copy-start(bf16[7168,144]{0,1:T(8,128)(2,1)} %param.21) | copy-start | bytes 6193156
  200.2 12.1 %copy-start.5 = (f32[7168]{0:T(1024)S(1)}, f32[7168]{0:T(1024)}, u32[]{:S(2)}) copy-start(f32[7168]{0:T(1024)} %param.20) | copy-start | bytes 86020
  211.6 0.7 copy-start.1
  217.6 18.0 %copy-start.6 = (u32[256]{0:T(256)S(1)}, u32[256]{0:T(256)}, u32[]{:S(2)}) copy-start(u32[256]{0:T(256)} %constant.55) | copy-start | bytes 3076
  222.0 55.1 %reduce-scatter.5.cloned.1.call-start = ((), (), s32[]{:S(2)}) async-start(), calls=%async_computation.5 | async-start | bytes 294912 | tf_op jit(solution)/shard_map/reduce_scatter | solution.py:31
Sparse Core Ops, SparseCore 0:
  72.6 127.5 all-gather.2
  222.1 13.3 reduce-scatter.2
  238.0 39.0 reduce-scatter.4
